TPU v7x, 128 devices: a whole 4x4x4 slice. The times are simulated.
128 devices in a mesh: dp: 1, cp: 128 (over z, y, x, core).
Axes of the slice: x: 4, y: 4, z: 4, core: 2. Of those that a mesh axis runs over, the one named last changes fastest.
Arguments:
- latent: bfloat16 [512, 48, 96, 128], P(('dp', 'cp'))
- conv_kernels: bfloat16 [4, 3, 3, 3, 128, 128], replicated
- conv_biases: float32 [4, 128], replicated
- gn_gammas: float32 [4, 128], replicated
- gn_betas: float32 [4, 128], replicated
Outputs:
- output: bfloat16 [512, 48, 96, 128], P(('dp', 'cp'))
All inputs are finite; a program needn't handle non-finite values.
Results may differ from a plain program's by a relative error of at most 0.0138496.
Values are sent between devices in bfloat16 or wider.
A program may use at most 1 GiB of HBM per device.

v0:
```python
import jax
import jax.numpy as jnp
from jax import lax
from jax.sharding import PartitionSpec as P

GROUPS = 32
NORM_EPS = 1e-6


def group_sums(hidden):
    n_frames, n_rows, n_cols, n_chans = hidden.shape
    grouped = hidden.astype(jnp.float32).reshape(n_frames, n_rows, n_cols, GROUPS, n_chans // GROUPS)
    return jnp.stack([jnp.sum(grouped, axis=(0, 1, 2, 4)), jnp.sum(grouped * grouped, axis=(0, 1, 2, 4))])


def norm_act(hidden, grp_sums, elem_count, gn_gamma, gn_beta):
    grp_mean = grp_sums[0] / elem_count
    grp_var = grp_sums[1] / elem_count - grp_mean * grp_mean
    group_width = hidden.shape[-1] // GROUPS
    chan_scale = jnp.repeat(lax.rsqrt(grp_var + NORM_EPS), group_width) * gn_gamma
    chan_shift = gn_beta - jnp.repeat(grp_mean, group_width) * chan_scale
    normed = (hidden.astype(jnp.float32) * chan_scale + chan_shift).astype(jnp.bfloat16)
    return jax.nn.silu(normed.astype(jnp.float32)).astype(jnp.bfloat16)


def conv_frames(padded, kernel, conv_bias):
    result = lax.conv_general_dilated(padded[None], kernel, window_strides=(1, 1, 1), padding=((0, 0), (1, 1), (1, 1)), dimension_numbers=("NDHWC", "DHWIO", "NDHWC"), preferred_element_type=jnp.float32)[0]
    return (result + conv_bias).astype(jnp.bfloat16)


def solution(mesh):
    n_time = mesh.shape["cp"]
    next_perm = [(src, src + 1) for src in range(n_time - 1)]
    frame_spec = P(("dp", "cp"))

    def local_fn(latent, conv_kernels, conv_biases, gn_gammas, gn_betas):
        n_frames, n_rows, n_cols, n_chans = latent.shape
        my_rank = lax.axis_index("cp")
        elem_count = n_time * n_frames * n_rows * n_cols * (n_chans // GROUPS)

        def gn_step(hidden, layer_idx):
            grp_sums = lax.psum(group_sums(hidden), "cp")
            return norm_act(hidden, grp_sums, elem_count, gn_gammas[layer_idx], gn_betas[layer_idx])

        def conv_step(act_in, layer_idx):
            from_prev = lax.ppermute(act_in[n_frames - 2:], "cp", next_perm)
            own_first = jnp.concatenate([act_in[:1], act_in[:1]], axis=0)
            halo_frames = jnp.where(my_rank == 0, own_first, from_prev)
            return conv_frames(jnp.concatenate([halo_frames, act_in], axis=0), conv_kernels[layer_idx], conv_biases[layer_idx])

        hidden = latent
        for block_idx in range(2):
            first_layer = 2 * block_idx
            inner = conv_step(gn_step(hidden, first_layer), first_layer)
            inner = conv_step(gn_step(inner, first_layer + 1), first_layer + 1)
            hidden = (hidden.astype(jnp.float32) + inner.astype(jnp.float32)).astype(jnp.bfloat16)
        return hidden

    return jax.shard_map(local_fn, mesh=mesh, in_specs=(frame_spec, P(), P(), P(), P()), out_specs=frame_spec, check_vma=False)
```

profile of v0, /device:TPU:1, one launch (start us, length us, event | category | flops | bytes accessed | tf_op | source)
XLA Modules:
  0.0 688.3 jit_solution(2501745096942043309)
XLA Ops:
  0.0 4.8 convert_reduce_fusion.1
  5.0 0.1 reduce_sum.97
  5.1 0.1 reduce_sum.100
  5.2 68.7 %psum.28 = f32[2,32]{1,0:T(2,128)S(1)} all-reduce(f32[2,32]{1,0:T(2,128)S(1)} %pad_maximum_fusion), channel_id=1, replica_groups=mesh['dp'=1,'cp'=128] {'cp'}, use_global_device_ids=true, to_apply=%region_4.5 | all-reduce | flops 64 | bytes 512 | tf_op jit(solution)/shard_map/psum | solution.py:42
  74.0 0.1 reshape.170
  74.3 0.7 bitcast_subtract_fusion.6
  75.0 4.9 fusion.13
  80.0 2.1 slice.141
  82.1 2.8 collective-permute-start
  85.0 0.6 slice_bitcast_fusion.4
  85.6 24.8 %collective-permute-done = bf16[2,48,96,128]{3,1,2,0:T(8,128)(2,1)} collective-permute-done((bf16[2,48,96,128]{3,1,2,0:T(8,128)(2,1)}, bf16[2,48,96,128]{3,1,2,0:T(8,128)(2,1)}, u32[]{:S(2)}, u32[]{:S(2)}) %collective-permute-start) | collective-permute-done | bytes 2359328 | tf_op jit(solution)/shard_map/ppermute | solution.py:46
  110.4 2.0 maximum_select_fusion
  112.4 3.5 maximum_bitcast_fusion
  115.9 4.3 pad
  120.2 5.0 copy.8
  125.3 1.6 slice.142
  126.9 42.1 %fusion.4 = (f32[128]{0:T(128)S(1)}, f32[128]{0:T(128)S(1)}, f32[4,48,8,13,128]{4,2,3,1,0:T(8,128)}) fusion(pred[8,13]{0,1:T(8,128)(4,1)S(1)} %copy-done.8, f32[128]{0:T(128)S(1)} %get-tuple-element.24, bf16[4,3,3,3,128,128]{5,4,3,2,1,0:T(8,128)(2,1)} %param.6, bf16[6,48,1,7,2,128]{5,3,4,1,0,2:T(8,128)(2,1)S(1)} %slice.142, ...), kind=kOutput, calls=%fused_computation.25 | convolution fusion | flops 17470586880 | bytes 19809896 | tf_op jit(solution)/shard_map/conv_general_dilated | solution.py:27
  169.1 0.1 reduce_sum.106
  169.3 0.1 reduce_sum.112
  169.5 67.5 %psum.29 = f32[2,32]{1,0:T(2,128)S(1)} all-reduce(f32[2,32]{1,0:T(2,128)S(1)} %pad_maximum_fusion.1), channel_id=1, replica_groups=mesh['dp'=1,'cp'=128] {'cp'}, use_global_device_ids=true, to_apply=%region_9.10 | all-reduce | flops 64 | bytes 512 | tf_op jit(solution)/shard_map/psum | solution.py:42
  237.4 5.7 copy.9
  243.2 2.8 fusion.17
  246.0 0.4 slice.145
  246.4 3.0 collective-permute-start.1
  249.5 25.3 %collective-permute-done.1 = bf16[2,48,96,128]{3,1,2,0:T(8,128)(2,1)S(1)} collective-permute-done((bf16[2,48,96,128]{3,1,2,0:T(8,128)(2,1)S(1)}, bf16[2,48,96,128]{3,1,2,0:T(8,128)(2,1)S(1)}, u32[]{:S(2)}, u32[]{:S(2)}) %collective-permute-start.1) | collective-permute-done | bytes 2359328 | tf_op jit(solution)/shard_map/ppermute | solution.py:46
  274.8 0.3 maximum_select_fusion.1
  275.1 3.5 maximum_bitcast_fusion.1
  278.6 4.3 pad.2
  282.9 5.0 copy.11
  288.0 1.6 slice.146
  289.6 41.8 %broadcast_select_fusion.2 = f32[4,48,8,13,128]{4,2,3,1,0:T(8,128)} fusion(pred[8,13]{0,1:T(8,128)(4,1)S(1)} %copy-done.8, bf16[6,48,1,7,2,128]{5,3,4,1,0,2:T(8,128)(2,1)S(1)} %slice.146, bf16[6,48,1,8,13,128]{5,3,4,1,0,2:T(8,128)(2,1)} %copy.11, bf16[4,3,3,3,128,128]{5,4,3,2,1,0:T(8,128)(2,1)} %param.6), kind=kOutput, calls=%fused_computation.101 | convolution fusion | flops 17450139648 | bytes 19808360 | tf_op jit(solution)/shard_map/conv_general_dilated | solution.py:27
  331.4 5.7 copy.12
  337.2 4.1 convert_reduce_fusion
  341.3 0.1 reduce_sum.115
  341.6 0.1 reduce_sum.145
  341.7 68.3 %psum.30 = f32[2,32]{1,0:T(2,128)S(1)} all-reduce(f32[2,32]{1,0:T(2,128)S(1)} %pad_maximum_fusion.2), channel_id=1, replica_groups=mesh['dp'=1,'cp'=128] {'cp'}, use_global_device_ids=true, to_apply=%region_14.15 | all-reduce | flops 64 | bytes 512 | tf_op jit(solution)/shard_map/psum | solution.py:42
  410.3 4.5 fusion.21
  414.8 0.4 slice.149
  415.2 2.6 collective-permute-start.2
  417.9 25.7 %collective-permute-done.2 = bf16[2,48,96,128]{3,1,2,0:T(8,128)(2,1)S(1)} collective-permute-done((bf16[2,48,96,128]{3,1,2,0:T(8,128)(2,1)S(1)}, bf16[2,48,96,128]{3,1,2,0:T(8,128)(2,1)S(1)}, u32[]{:S(2)}, u32[]{:S(2)}) %collective-permute-start.2) | collective-permute-done | bytes 2359328 | tf_op jit(solution)/shard_map/ppermute | solution.py:46
  443.6 0.3 maximum_select_fusion.2
  443.9 3.5 maximum_bitcast_fusion.2
  447.4 4.3 pad.4
  451.7 5.0 copy.14
  456.8 1.6 slice.150
  458.4 42.1 %fusion.7 = (f32[128]{0:T(128)S(1)}, f32[128]{0:T(128)S(1)}, f32[4,48,8,13,128]{4,2,3,1,0:T(8,128)}) fusion(pred[8,13]{0,1:T(8,128)(4,1)S(1)} %copy-done.8, f32[128]{0:T(128)S(1)} %copy-done.3, bf16[4,3,3,3,128,128]{5,4,3,2,1,0:T(8,128)(2,1)} %param.6, bf16[6,48,1,7,2,128]{5,3,4,1,0,2:T(8,128)(2,1)S(1)} %slice.150, bf16[6,48,1,8,13,128]{5,3,4,1,0,2:T(8,128)(2,1)} %copy.14), kind=kOutput, calls=%fused_computation.28 | convolution fusion | flops 17470586880 | bytes 19809896 | tf_op jit(solution)/shard_map/conv_general_dilated | solution.py:27
  500.6 0.1 reduce_sum.148
  500.8 0.1 reduce_sum.151
  500.9 68.3 %psum.31 = f32[2,32]{1,0:T(2,128)S(1)} all-reduce(f32[2,32]{1,0:T(2,128)S(1)} %pad_maximum_fusion.3), channel_id=1, replica_groups=mesh['dp'=1,'cp'=128] {'cp'}, use_global_device_ids=true, to_apply=%region_19.20 | all-reduce | flops 64 | bytes 512 | tf_op jit(solution)/shard_map/psum | solution.py:42
  569.3 0.1 reshape.176
  569.6 5.7 copy.15
  575.4 2.8 fusion.25
  578.2 0.4 slice.153
  578.6 2.6 collective-permute-start.3
  581.3 25.7 %collective-permute-done.3 = bf16[2,48,96,128]{3,1,2,0:T(8,128)(2,1)S(1)} collective-permute-done((bf16[2,48,96,128]{3,1,2,0:T(8,128)(2,1)S(1)}, bf16[2,48,96,128]{3,1,2,0:T(8,128)(2,1)S(1)}, u32[]{:S(2)}, u32[]{:S(2)}) %collective-permute-start.3) | collective-permute-done | bytes 2359328 | tf_op jit(solution)/shard_map/ppermute | solution.py:46
  606.9 0.3 maximum_select_fusion.3
  607.2 3.5 maximum_bitcast_fusion.3
  610.8 7.3 %pad.6 = bf16[6,48,1,104,128]{4,1,3,0,2:T(8,128)(2,1)} pad(bf16[6,48,1,96,128]{4,1,3,0,2:T(8,128)(2,1)} %maximum_bitcast_fusion.3, bf16[]{:T(256)} %constant.27), padding=0_0x0_0x0_0x1_7x0_0 | pad | bytes 14745602 | tf_op jit(solution)/shard_map/broadcast_in_dim | solution.py:27
  618.1 8.4 %copy.17 = bf16[6,48,1,8,13,128]{5,3,4,1,0,2:T(8,128)(2,1)} copy(bf16[6,48,1,8,13,128]{5,1,4,3,0,2:T(8,128)(2,1)} %bitcast.173) | data formatting | bytes 15335424 | tf_op jit(solution)/shard_map/conv_general_dilated | solution.py:27
  626.5 1.6 slice.154
  628.1 41.9 %broadcast_select_fusion = f32[4,48,8,13,128]{4,2,3,1,0:T(8,128)} fusion(pred[8,13]{0,1:T(8,128)(4,1)S(1)} %copy-done.8, bf16[6,48,1,7,2,128]{5,3,4,1,0,2:T(8,128)(2,1)S(1)} %slice.154, bf16[6,48,1,8,13,128]{5,3,4,1,0,2:T(8,128)(2,1)} %copy.17, bf16[4,3,3,3,128,128]{5,4,3,2,1,0:T(8,128)(2,1)} %param.6), kind=kOutput, calls=%fused_computation.99 | convolution fusion | flops 17450139648 | bytes 19808360 | tf_op jit(solution)/shard_map/conv_general_dilated | solution.py:27
  670.0 9.5 %copy.18 = f32[4,48,8,13,128]{4,1,3,2,0:T(8,128)} copy(f32[4,48,8,13,128]{4,2,3,1,0:T(8,128)} %broadcast_select_fusion) | data formatting | bytes 20447232 | tf_op jit(solution)/shard_map/conv_general_dilated | solution.py:27
  679.6 5.0 fusion.33
  684.6 3.4 copy.19
  (69 shorter events, 2.5 us)
Async XLA Ops:
  4.8 80.2 %copy-start.5 = (f32[4,128]{1,0:T(4,128)S(1)}, f32[4,128]{1,0:T(4,128)}, u32[]{:S(2)}) copy-start(f32[4,128]{1,0:T(4,128)} %param.7) | copy-start | bytes 6148
  80.0 4.9 copy-start
  82.1 28.3 %collective-permute-start = (bf16[2,48,96,128]{3,1,2,0:T(8,128)(2,1)}, bf16[2,48,96,128]{3,1,2,0:T(8,128)(2,1)}, u32[]{:S(2)}, u32[]{:S(2)}) collective-permute-start(bf16[2,48,96,128]{3,1,2,0:T(8,128)(2,1)} %slice.141), channel_id=1, source_target_pairs={{0,1},{1,2},{2,3},{3,4},{4,5},{5,6},{6,7},{7,8},{8,9},{9,10},{10,1... | collective-permute-start | bytes 7077896 | tf_op jit(solution)/shard_map/ppermute | solution.py:46
  85.0 27.4 %copy-start.1 = (bf16[4,48,96,128]{3,1,2,0:T(8,128)(2,1)S(1)}, bf16[4,48,96,128]{3,1,2,0:T(8,128)(2,1)}, u32[]{:S(2)}) copy-start(bf16[4,48,96,128]{3,1,2,0:T(8,128)(2,1)} %copy-done) | copy-start | bytes 14155780
  120.2 6.7 copy-start.8
  237.4 5.8 copy-start.6
  237.4 5.8 copy-start.7
  246.4 28.4 %collective-permute-start.1 = (bf16[2,48,96,128]{3,1,2,0:T(8,128)(2,1)S(1)}, bf16[2,48,96,128]{3,1,2,0:T(8,128)(2,1)S(1)}, u32[]{:S(2)}, u32[]{:S(2)}) collective-permute-start(bf16[2,48,96,128]{3,1,2,0:T(8,128)(2,1)S(1)} %slice.145), channel_id=1, source_target_pairs={{0,1},{1,2},{2,3},{3,4},{4,5},{5,6},{6,7},{7,8},{8,9},{9,10},{10,1... | collective-permute-start | bytes 7077896 | tf_op jit(solution)/shard_map/ppermute | solution.py:46
  282.9 54.2 %slice-start = ((s8[4718592]{0:T(1024)(128)(4,1)}), s8[524288]{0:T(1024)(128)(4,1)S(1)}, s32[]{:S(2)}) async-start(s8[4718592]{0:T(1024)(128)(4,1)} %bitcast.165), calls=%async_computation | async-start | bytes 1048576
  289.6 47.6 %slice-start.1 = ((s8[4718592]{0:T(1024)(128)(4,1)}), s8[4194304]{0:T(1024)(128)(4,1)S(1)}, s32[]{:S(2)}) async-start(s8[4718592]{0:T(1024)(128)(4,1)} %bitcast.165), calls=%async_computation.1 | async-start | bytes 8388608
  331.4 5.7 copy-start.4
  415.2 28.4 %collective-permute-start.2 = (bf16[2,48,96,128]{3,1,2,0:T(8,128)(2,1)S(1)}, bf16[2,48,96,128]{3,1,2,0:T(8,128)(2,1)S(1)}, u32[]{:S(2)}, u32[]{:S(2)}) collective-permute-start(bf16[2,48,96,128]{3,1,2,0:T(8,128)(2,1)S(1)} %slice.149), channel_id=1, source_target_pairs={{0,1},{1,2},{2,3},{3,4},{4,5},{5,6},{6,7},{7,8},{8,9},{9,10},{10,1... | collective-permute-start | bytes 7077896 | tf_op jit(solution)/shard_map/ppermute | solution.py:46
  451.7 6.7 copy-start.3
  578.6 28.3 %collective-permute-start.3 = (bf16[2,48,96,128]{3,1,2,0:T(8,128)(2,1)S(1)}, bf16[2,48,96,128]{3,1,2,0:T(8,128)(2,1)S(1)}, u32[]{:S(2)}, u32[]{:S(2)}) collective-permute-start(bf16[2,48,96,128]{3,1,2,0:T(8,128)(2,1)S(1)} %slice.153), channel_id=1, source_target_pairs={{0,1},{1,2},{2,3},{3,4},{4,5},{5,6},{6,7},{7,8},{8,9},{9,10},{10,1... | collective-permute-start | bytes 7077896 | tf_op jit(solution)/shard_map/ppermute | solution.py:46
  618.1 61.5 %slice-start.2 = ((s8[4718592]{0:T(1024)(128)(4,1)}), s8[4194304]{0:T(1024)(128)(4,1)S(1)}, s32[]{:S(2)}) async-start(s8[4718592]{0:T(1024)(128)(4,1)} %bitcast.167), calls=%async_computation.2 | async-start | bytes 8388608
  628.1 51.5 %slice-start.3 = ((s8[4718592]{0:T(1024)(128)(4,1)}), s8[524288]{0:T(1024)(128)(4,1)S(1)}, s32[]{:S(2)}) async-start(s8[4718592]{0:T(1024)(128)(4,1)} %bitcast.167), calls=%async_computation.3 | async-start | bytes 1048576
  670.0 9.5 %copy-start.2 = (f32[128]{0:T(128)S(1)}, f32[128]{0:T(128)}, u32[]{:S(2)}) copy-start(f32[128]{0:T(128)} %get-tuple-element.22) | copy-start | bytes 1540
where the time goes:
time: 698 us; the launch traced here: 688 us
  blocking collectives  273 us (39%)
  matrix products  168 us (24%)
  waiting for transfers between devices  101 us (14%)
  local copies, waits for them, and re-layouts  86.7 us (12%)
  other arithmetic  47.6 us (7%)
  starting transfers between devices  11 us (2%)
    psum x4, blocking collectives, gn_step(): grp_sums = lax.psum(group_sums(hidden), 'cp')  273 us
    conv_general_dilated x4, matrix products, conv_frames(): lax.conv_general_dilated(padded[None], kernel, window_strides=(1, 1, 1),...  168 us
    ppermute x4, waiting for transfers between devices, conv_step(): from_prev = lax.ppermute(act_in[n_frames - 2:], 'cp', next_perm)  101 us
    conv_general_dilated x12, local copies, waits for them, and re-layouts, conv_frames(): lax.conv_general_dilated(padded[None], kernel, window_strides=(1, 1, 1),...  56.6 us
    broadcast_in_dim x4, local copies, waits for them, and re-layouts, conv_frames(): padded[None]  20.2 us
    convert_element_type x4, other arithmetic, norm_act(): return jax.nn.silu(normed.astype(jnp.float32)).astype(jnp.bfloat16)  15 us
    broadcast_in_dim x4, other arithmetic, conv_frames(): padded[None]  14.1 us
  transfers between devices with their start and end apart: 4, of which 4 were waited for; matrix products, arithmetic and copies ran while one was open for 0% of the time, Pallas kernels for 0%

commit v1 on v0

v1 whole, which is shorter than its diff:
```python
import functools

import jax
import jax.numpy as jnp
from jax import lax
from jax.experimental import pallas as pl
from jax.experimental.pallas import tpu as pltpu
from jax.sharding import PartitionSpec as P

GROUP_WIDTH = 4
NORM_EPS = 1e-6
LAYERS = 4
NEAR = 8
ROWS = 6
UNROLL = 2
MESH = pl.DeviceIdType.MESH
BF16 = jnp.bfloat16
F32 = jnp.float32


def _plan():
    plan = []
    for out in range(2):
        pieces = [(out + k, di, ((k, di, 0), (k, di, 1))) for di in range(3) for k in range(3)]
        plan.append(pieces)
    pieces = []
    for di in range(3):
        for f in range(4):
            pieces.append((f, di, ((f, di, 2) if f < 3 else None, (f - 1, di, 2) if f > 0 else None)))
    plan.append(pieces)
    return plan


PLAN = _plan()


def kernel(n_dev, *refs):
    (lat, kern, bias, gamma, beta, out, cur, mid, act, halo, wts, part1, part2, gat1, gat2, coef, mid_sum, left_sum, right_sum, load_sem, wts_sem, out_sem, halo_send, halo_recv, send1, recv1, send2, recv2) = refs
    n_frames, height, width, chans = lat.shape
    far = n_dev // NEAR
    elem_count = float(n_dev * n_frames * height * width * GROUP_WIDTH)
    me = lax.axis_index("cp")
    near_pos = lax.rem(me, NEAR)
    far_pos = me // NEAR
    near_base = me - near_pos

    def near_peer(j):
        slot = lax.rem(near_pos + j, NEAR)
        return slot, near_base + slot

    def far_peer(j):
        slot = lax.rem(far_pos + j, far)
        return slot, slot * NEAR + near_pos

    barrier = pltpu.get_barrier_semaphore()
    for j in range(1, NEAR):
        pl.semaphore_signal(barrier, inc=1, device_id={"cp": near_peer(j)[1]}, device_id_type=MESH)
    for j in range(1, far):
        pl.semaphore_signal(barrier, inc=1, device_id={"cp": far_peer(j)[1]}, device_id_type=MESH)

    for device in (lax.rem(me + 1, n_dev), lax.rem(me + n_dev - 1, n_dev)):
        pl.semaphore_signal(barrier, inc=1, device_id={"cp": device}, device_id_type=MESH)

    frame_loads = [pltpu.make_async_copy(lat.at[f], cur.at[f], load_sem.at[f]) for f in range(n_frames)]
    for copy in frame_loads:
        copy.start()
    wts_loads = [pltpu.make_async_copy(kern.at[n], wts.at[n], wts_sem.at[n]) for n in range(LAYERS)]
    for copy in wts_loads:
        copy.start()

    pl.semaphore_wait(barrier, NEAR - 1 + far - 1 + 2)

    def halo_copy(src, slot):
        return pltpu.make_async_remote_copy(src_ref=src.at[pl.ds(n_frames - 2, 2)], dst_ref=halo.at[slot], send_sem=halo_send.at[slot], recv_sem=halo_recv.at[slot], device_id={"cp": me + 1}, device_id_type=MESH)

    @pl.when(me < n_dev - 1)
    def _():
        halo_copy(lat, 0).start()

    zero_row = jnp.zeros((width, chans), BF16)
    for f in range(n_frames + 2):
        act[f, 0] = zero_row
        act[f, height + 1] = zero_row
    edge = jnp.zeros((8, chans), F32)
    for r in range(ROWS):
        for o in range(2):
            left_sum[r, o, pl.ds(0, 8), :] = edge
            right_sum[r, o, pl.ds(width + 8, 8), :] = edge

    def row_sums(value):
        parts = value.reshape(width // 8, 8, chans)
        return jnp.sum(parts, axis=0), jnp.sum(parts * parts, axis=0)

    zero_sums = (jnp.zeros((8, chans), F32), jnp.zeros((8, chans), F32))

    def latent_sums(f, sums):
        def step(i, sums):
            for r in range(2):
                s1, s2 = row_sums(cur[f, 2 * i + r].astype(F32))
                sums = (sums[0] + s1, sums[1] + s2)
            return sums

        return lax.fori_loop(0, height // 2, step, sums)

    def group_total(sums):
        lane = lax.broadcasted_iota(jnp.int32, sums.shape, 1)
        for d in (1, 2):
            other = jnp.where(lax.rem(lane, 2 * d) < d, pltpu.roll(sums, chans - d, axis=1), pltpu.roll(sums, d, axis=1))
            sums = sums + other
        return sums

    def exchange(layer, size, pos, peer, part, gat, send, recv):
        def copy(j):
            slot, device = peer(j)
            return pltpu.make_async_remote_copy(src_ref=part, dst_ref=gat.at[layer, pos], send_sem=send.at[j], recv_sem=recv.at[layer, pos], device_id={"cp": device}, device_id_type=MESH)

        for j in range(1, size):
            copy(j).start()
        gat[layer, pos] = part[...]
        for j in range(1, size):
            slot, device = peer(j)
            pltpu.make_async_remote_copy(src_ref=part, dst_ref=gat.at[layer, slot], send_sem=send.at[j], recv_sem=recv.at[layer, slot], device_id={"cp": device}, device_id_type=MESH).wait_recv()
        total = gat[layer, 0]
        for slot in range(1, size):
            total = total + gat[layer, slot]
        for j in range(1, size):
            copy(j).wait_send()
        return total

    def norm_coefs(layer, sums):
        part1[...] = jnp.concatenate([jnp.sum(sums[0], axis=0, keepdims=True), jnp.sum(sums[1], axis=0, keepdims=True)], axis=0)
        part2[...] = exchange(layer, NEAR, near_pos, near_peer, part1, gat1, send1, recv1)
        total = exchange(layer, far, far_pos, far_peer, part2, gat2, send2, recv2)
        total = group_total(total)
        mean = total[0:1] / elem_count
        var = total[1:2] / elem_count - mean * mean
        scale = lax.rsqrt(var + NORM_EPS) * gamma[layer]
        coef[0] = scale
        coef[1] = beta[layer] - mean * scale

    def act_rows(value):
        normed = (value.astype(F32) * coef[0] + coef[1]).astype(BF16).astype(F32)
        half = normed * 0.5
        return (half + half * jnp.tanh(half)).astype(BF16)

    def act_frames(src, frames, first):
        def step(i, carry):
            for f in frames:
                for r in range(2):
                    act[first + f, 2 * i + r + 1] = act_rows(src[f, 2 * i + r])
            return carry

        lax.fori_loop(0, height // 2, step, 0)

    def conv_pair(layer, first, dst, residual, sums):
        shift = bias[layer]
        zero_tile = jnp.zeros((chans, chans), BF16)

        def tap(index):
            return zero_tile if index is None else wts[layer, index[0], index[1], index[2]]

        def block_pair(row):
            for kind, pieces in enumerate(PLAN):
                rhs = jnp.concatenate([jnp.concatenate([tap(t) for t in piece[2]], axis=1) for piece in pieces], axis=0)
                lhs = jnp.concatenate([act[first + f, pl.ds(row + di, ROWS)].reshape(ROWS * width, chans) for f, di, _ in pieces], axis=1)
                value = jnp.dot(lhs, rhs, preferred_element_type=F32).reshape(ROWS, width, 2 * chans)
                lo, hi = value[:, :, :chans], value[:, :, chans:]
                if kind < 2:
                    left_sum[:, kind, pl.ds(8, width), :] = lo
                    mid_sum[:, kind] = hi
                else:
                    right_sum[:, 0, pl.ds(8, width), :] = lo
                    right_sum[:, 1, pl.ds(8, width), :] = hi

        def finish(row, sums):
            for r in range(ROWS):
                for o in range(2):
                    value = mid_sum[r, o] + left_sum[r, o, pl.ds(7, width), :] + right_sum[r, o, pl.ds(9, width), :]
                    value = (value + shift).astype(BF16).astype(F32)
                    at = row + r
                    if residual:
                        value = (cur[first + o, at].astype(F32) + value).astype(BF16).astype(F32)
                    dst[first + o, at] = value.astype(BF16)
                    s1, s2 = row_sums(value)
                    sums = (sums[0] + s1, sums[1] + s2)
            return sums

        def step(i, sums):
            for u in range(UNROLL):
                row = (i * UNROLL + u) * ROWS
                block_pair(row)
                sums = finish(row, sums)
            return sums

        return lax.fori_loop(0, height // (ROWS * UNROLL), step, sums)

    def layer_step(block, odd, sums):
        layer = 2 * block + odd
        src, dst = (mid, cur) if odd else (cur, mid)
        norm_coefs(layer, sums)
        act_frames(src, range(n_frames), 2)
        sums = conv_pair(layer, 2, dst, odd == 1, zero_sums)

        def send_next():
            @pl.when(me < n_dev - 1)
            def _():
                halo_copy(dst, 1 - odd).start()

        if odd:

            @pl.when(block == 0)
            def _():
                send_next()

            @pl.when(block == 1)
            def _():
                pltpu.make_async_copy(cur.at[pl.ds(2, 2)], out.at[pl.ds(2, 2)], out_sem.at[1]).start()
        else:
            send_next()

        @pl.when(me == 0)
        def _():
            for f in range(2):
                def step(i, carry):
                    act[f, i + 1] = act[2, i + 1]
                    return carry

                lax.fori_loop(0, height, step, 0)

        @pl.when(me > 0)
        def _():
            halo_copy(src, odd).wait_recv()
            act_frames(halo.at[odd], range(2), 0)

        @pl.when(me < n_dev - 1)
        def _():
            halo_copy(src, odd).wait_send()

        return conv_pair(layer, 0, dst, odd == 1, sums)

    sums = zero_sums
    for f in range(n_frames):
        frame_loads[f].wait()
        sums = latent_sums(f, sums)
    for copy in wts_loads:
        copy.wait()

    def block_step(block, sums):
        return layer_step(block, 1, layer_step(block, 0, sums))

    lax.fori_loop(0, LAYERS // 2, block_step, sums)
    pltpu.make_async_copy(cur.at[pl.ds(0, 2)], out.at[pl.ds(0, 2)], out_sem.at[0]).start()
    pltpu.make_async_copy(cur.at[pl.ds(2, 2)], out.at[pl.ds(2, 2)], out_sem.at[1]).wait()
    pltpu.make_async_copy(cur.at[pl.ds(0, 2)], out.at[pl.ds(0, 2)], out_sem.at[0]).wait()


def solution(mesh):
    n_dev = mesh.shape["cp"]
    frame_spec = P(("dp", "cp"))

    def local_fn(latent, conv_kernels, conv_biases, gn_gammas, gn_betas):
        n_frames, height, width, chans = latent.shape
        far = n_dev // NEAR
        row = (LAYERS, 1, chans)
        vmem = pl.BlockSpec(memory_space=pltpu.VMEM)
        anywhere = pl.BlockSpec(memory_space=pl.ANY)
        dma = pltpu.SemaphoreType.DMA
        return pl.pallas_call(
            functools.partial(kernel, n_dev),
            out_shape=jax.ShapeDtypeStruct(latent.shape, BF16),
            in_specs=[anywhere, anywhere, vmem, vmem, vmem],
            out_specs=anywhere,
            scratch_shapes=[
                pltpu.VMEM(latent.shape, BF16),
                pltpu.VMEM(latent.shape, BF16),
                pltpu.VMEM((n_frames + 2, height + 2, width, chans), BF16),
                pltpu.VMEM((2, 2, height, width, chans), BF16),
                pltpu.VMEM(conv_kernels.shape, BF16),
                pltpu.VMEM((2, chans), F32),
                pltpu.VMEM((2, chans), F32),
                pltpu.VMEM((LAYERS, NEAR, 2, chans), F32),
                pltpu.VMEM((LAYERS, far, 2, chans), F32),
                pltpu.VMEM((2, 1, chans), F32),
                pltpu.VMEM((ROWS, 2, width, chans), F32),
                pltpu.VMEM((ROWS, 2, width + 16, chans), F32),
                pltpu.VMEM((ROWS, 2, width + 16, chans), F32),
                dma((n_frames,)),
                dma((LAYERS,)),
                dma((2,)),
                dma((2,)),
                dma((2,)),
                dma((NEAR,)),
                dma((LAYERS, NEAR)),
                dma((far,)),
                dma((LAYERS, far)),
            ],
            compiler_params=pltpu.CompilerParams(collective_id=0, has_side_effects=True, vmem_limit_bytes=60 * 1024 * 1024),
            name="resblocks",
        )(latent, conv_kernels, conv_biases.reshape(row), gn_gammas.reshape(row), gn_betas.reshape(row))

    return jax.shard_map(local_fn, mesh=mesh, in_specs=(frame_spec, P(), P(), P(), P()), out_specs=frame_spec, check_vma=False)
```

time: 698 us -> 214 us (0.31); the launches traced: 688 us -> 214 us
  blocking collectives: 273 us -> 0 us
  Pallas kernels: 0 us -> 208 us
  matrix products: 168 us -> 0 us
  waiting for transfers between devices: 101 us -> 0 us
  local copies, waits for them, and re-layouts: 86.7 us -> 5.51 us
  other arithmetic: 47.6 us -> 0 us
  starting transfers between devices: 11 us -> 0 us
    psum x4 -> x0, blocking collectives: 273 us -> none  [gn_step(): grp_sums = lax.psum(group_sums(hidden), 'cp')]
    pallas_call x0 -> x1, Pallas kernels: none -> 208 us  [local_fn(): pl.pallas_call(functools.partial(kernel, n_dev), out_shape=jax.ShapeDtype...]
    conv_general_dilated x4 -> x0, matrix products: 168 us -> none  [conv_frames(): lax.conv_general_dilated(padded[None], kernel, window_strides=(1, 1, 1),...]
    ppermute x4 -> x0, waiting for transfers between devices: 101 us -> none  [conv_step(): from_prev = lax.ppermute(act_in[n_frames - 2:], 'cp', next_perm)]
    conv_general_dilated x12 -> x0, local copies, waits for them, and re-layouts: 56.6 us -> none  [conv_frames(): lax.conv_general_dilated(padded[None], kernel, window_strides=(1, 1, 1),...]
    broadcast_in_dim x12 -> x0, local copies, waits for them, and re-layouts: 20.8 us -> none  [the longest x4 20.2 us: conv_frames(): padded[None]]
    convert_element_type x5 -> x0, other arithmetic: 20 us -> none  [the longest x4 15 us: norm_act(): return jax.nn.silu(normed.astype(jnp.float32)).astype(jnp.bfloat16)]
    broadcast_in_dim x4 -> x0, other arithmetic: 14.1 us -> none  [conv_frames(): padded[None]]
  transfers between devices with their start and end apart: 4 -> 0, of which waited for: 4 -> 0; matrix products, arithmetic and copies ran while one was open for 0% -> 0% of each run, Pallas kernels for 0% -> 0%
where the time goes in v1:
time: 214 us
  Pallas kernels  208 us (97%)
  local copies, waits for them, and re-layouts  5.51 us (3%)
    pallas_call x1, Pallas kernels, local_fn(): pl.pallas_call(functools.partial(kernel, n_dev), out_shape=jax.ShapeDtype...  208 us
    unnamed x1, local copies, waits for them, and re-layouts  5.51 us

profile of v1, /device:TPU:1, one launch (start us, length us, event | category | flops | bytes accessed | tf_op | source)
XLA Modules:
  0.0 213.6 jit_solution(2381796778208040921)
XLA Ops:
  0.0 208.1 %resblocks.1 = bf16[4,48,96,128]{3,2,1,0:T(8,128)(2,1)} custom-call(bf16[4,48,96,128]{3,2,1,0:T(8,128)(2,1)} %refs_0_.1, bf16[4,3,3,3,128,128]{5,4,3,2,1,0:T(8,128)(2,1)} %refs_1_.1, f32[4,1,128]{2,1,0:T(1,128)} %bitcast.3, f32[4,1,128]{2,1,0:T(1,128)} %bitcast.4, f32[4,1,128]{2,1,0:T(1,128)} %bitcast.5), custom_call_target="tpu_custom_call" | custom-call | tf_op jit(solution)/shard_map/resblocks/pallas_call | solution.py:268
  208.1 5.5 %copy.7 = bf16[4,48,96,128]{3,2,1,0:T(8,128)(2,1)} copy(bf16[4,48,96,128]{3,2,1,0:T(8,128)(2,1)} %resblocks.1) | data formatting | bytes 9437184

commit v2 on v1

--- a/solution.py
+++ b/solution.py
@@ -10,7 +10,8 @@
 GROUP_WIDTH = 4
 NORM_EPS = 1e-6
 LAYERS = 4
-NEAR = 8
+LINE = 4
+NEAR = 2 * LINE
 ROWS = 6
 UNROLL = 2
 MESH = pl.DeviceIdType.MESH
@@ -35,7 +36,7 @@
 
 
 def kernel(n_dev, *refs):
-    (lat, kern, bias, gamma, beta, out, cur, mid, act, halo, wts, part1, part2, gat1, gat2, coef, mid_sum, left_sum, right_sum, load_sem, wts_sem, out_sem, halo_send, halo_recv, send1, recv1, send2, recv2) = refs
+    (lat, kern, bias, gamma, beta, out, cur, mid, act, halo, wts, part0, part1, part2, gat0, gat1, gat2, coef, mid_sum, left_sum, right_sum, load_sem, wts_sem, out_sem, halo_send, halo_recv, send0, recv0, send1, recv1, send2, recv2) = refs
     n_frames, height, width, chans = lat.shape
     far = n_dev // NEAR
     elem_count = float(n_dev * n_frames * height * width * GROUP_WIDTH)
@@ -43,10 +44,9 @@
     near_pos = lax.rem(me, NEAR)
     far_pos = me // NEAR
     near_base = me - near_pos
-
-    def near_peer(j):
-        slot = lax.rem(near_pos + j, NEAR)
-        return slot, near_base + slot
+    core = lax.rem(me, 2)
+    line_pos = near_pos // 2
+    partner = me + 1 - 2 * core
 
     def far_peer(j):
         slot = lax.rem(far_pos + j, far)
@@ -54,7 +54,7 @@
 
     barrier = pltpu.get_barrier_semaphore()
     for j in range(1, NEAR):
-        pl.semaphore_signal(barrier, inc=1, device_id={"cp": near_peer(j)[1]}, device_id_type=MESH)
+        pl.semaphore_signal(barrier, inc=1, device_id={"cp": near_base + lax.rem(near_pos + j, NEAR)}, device_id_type=MESH)
     for j in range(1, far):
         pl.semaphore_signal(barrier, inc=1, device_id={"cp": far_peer(j)[1]}, device_id_type=MESH)
 
@@ -109,28 +109,63 @@
             sums = sums + other
         return sums
 
-    def exchange(layer, size, pos, peer, part, gat, send, recv):
-        def copy(j):
-            slot, device = peer(j)
-            return pltpu.make_async_remote_copy(src_ref=part, dst_ref=gat.at[layer, pos], send_sem=send.at[j], recv_sem=recv.at[layer, pos], device_id={"cp": device}, device_id_type=MESH)
-
-        for j in range(1, size):
-            copy(j).start()
-        gat[layer, pos] = part[...]
-        for j in range(1, size):
-            slot, device = peer(j)
-            pltpu.make_async_remote_copy(src_ref=part, dst_ref=gat.at[layer, slot], send_sem=send.at[j], recv_sem=recv.at[layer, slot], device_id={"cp": device}, device_id_type=MESH).wait_recv()
+    def remote(src, dst, send, recv, device):
+        return pltpu.make_async_remote_copy(src_ref=src, dst_ref=dst, send_sem=send, recv_sem=recv, device_id={"cp": device}, device_id_type=MESH)
+
+    def in_order(gat, layer, size):
         total = gat[layer, 0]
         for slot in range(1, size):
             total = total + gat[layer, slot]
-        for j in range(1, size):
-            copy(j).wait_send()
         return total
 
+    def chip_sum(layer):
+        copy = remote(part0, gat0.at[layer], send0, recv0.at[layer], partner)
+        copy.start()
+        copy.wait()
+        return part0[...] + gat0[layer]
+
+    def line_sum(layer):
+        def copies():
+            for j in range(1, LINE):
+                slot = lax.rem(line_pos + j, LINE)
+                for c in range(2):
+                    yield remote(part1, gat1.at[layer, line_pos], send1.at[j, c], recv1.at[layer, line_pos], near_base + 2 * slot + c)
+
+        @pl.when(core == 0)
+        def _():
+            for copy in copies():
+                copy.start()
+
+        gat1[layer, line_pos] = part1[...]
+        for j in range(1, LINE):
+            slot = lax.rem(line_pos + j, LINE)
+            remote(part1, gat1.at[layer, slot], send1.at[j, 0], recv1.at[layer, slot], me).wait_recv()
+        total = in_order(gat1, layer, LINE)
+
+        @pl.when(core == 0)
+        def _():
+            for copy in copies():
+                copy.wait_send()
+
+        return total
+
+    def far_sum(layer):
+        for j in range(1, far):
+            remote(part2, gat2.at[layer, far_pos], send2.at[j], recv2.at[layer, far_pos], far_peer(j)[1]).start()
+        gat2[layer, far_pos] = part2[...]
+        for j in range(1, far):
+            slot, device = far_peer(j)
+            remote(part2, gat2.at[layer, slot], send2.at[j], recv2.at[layer, slot], device).wait_recv()
+        total = in_order(gat2, layer, far)
+        for j in range(1, far):
+            remote(part2, gat2.at[layer, far_pos], send2.at[j], recv2.at[layer, far_pos], far_peer(j)[1]).wait_send()
+        return total
+
     def norm_coefs(layer, sums):
-        part1[...] = jnp.concatenate([jnp.sum(sums[0], axis=0, keepdims=True), jnp.sum(sums[1], axis=0, keepdims=True)], axis=0)
-        part2[...] = exchange(layer, NEAR, near_pos, near_peer, part1, gat1, send1, recv1)
-        total = exchange(layer, far, far_pos, far_peer, part2, gat2, send2, recv2)
+        part0[...] = jnp.concatenate([jnp.sum(sums[0], axis=0, keepdims=True), jnp.sum(sums[1], axis=0, keepdims=True)], axis=0)
+        part1[...] = chip_sum(layer)
+        part2[...] = line_sum(layer)
+        total = far_sum(layer)
         total = group_total(total)
         mean = total[0:1] / elem_count
         var = total[1:2] / elem_count - mean * mean
@@ -278,7 +313,9 @@
                 pltpu.VMEM(conv_kernels.shape, BF16),
                 pltpu.VMEM((2, chans), F32),
                 pltpu.VMEM((2, chans), F32),
-                pltpu.VMEM((LAYERS, NEAR, 2, chans), F32),
+                pltpu.VMEM((2, chans), F32),
+                pltpu.VMEM((LAYERS, 2, chans), F32),
+                pltpu.VMEM((LAYERS, LINE, 2, chans), F32),
                 pltpu.VMEM((LAYERS, far, 2, chans), F32),
                 pltpu.VMEM((2, 1, chans), F32),
                 pltpu.VMEM((ROWS, 2, width, chans), F32),
@@ -289,8 +326,10 @@
                 dma((2,)),
                 dma((2,)),
                 dma((2,)),
-                dma((NEAR,)),
-                dma((LAYERS, NEAR)),
+                dma,
+                dma((LAYERS,)),
+                dma((LINE, 2)),
+                dma((LAYERS, LINE)),
                 dma((far,)),
                 dma((LAYERS, far)),
             ],

time: 214 us -> 200 us (0.935)
  Pallas kernels: 208 us -> 195 us
    pallas_call x1, Pallas kernels: 208 us -> 195 us  [local_fn(): pl.pallas_call(functools.partial(kernel, n_dev), out_shape=jax.ShapeDtype...]
where the time goes in v2:
time: 200 us
  Pallas kernels  195 us (98%)
  local copies, waits for them, and re-layouts  5.51 us (3%)
    pallas_call x1, Pallas kernels, local_fn(): pl.pallas_call(functools.partial(kernel, n_dev), out_shape=jax.ShapeDtype...  195 us
    unnamed x1, local copies, waits for them, and re-layouts  5.51 us

profile of v2, /device:TPU:1, one launch (start us, length us, event | category | flops | bytes accessed | tf_op | source)
XLA Modules:
  0.0 200.0 jit_solution(16189373133827099658)
XLA Ops:
  0.0 194.5 %resblocks.1 = bf16[4,48,96,128]{3,2,1,0:T(8,128)(2,1)} custom-call(bf16[4,48,96,128]{3,2,1,0:T(8,128)(2,1)} %refs_0_.1, bf16[4,3,3,3,128,128]{5,4,3,2,1,0:T(8,128)(2,1)} %refs_1_.1, f32[4,1,128]{2,1,0:T(1,128)} %bitcast.3, f32[4,1,128]{2,1,0:T(1,128)} %bitcast.4, f32[4,1,128]{2,1,0:T(1,128)} %bitcast.5), custom_call_target="tpu_custom_call" | custom-call | tf_op jit(solution)/shard_map/resblocks/pallas_call | solution.py:303
  194.5 5.5 %copy.7 = bf16[4,48,96,128]{3,2,1,0:T(8,128)(2,1)} copy(bf16[4,48,96,128]{3,2,1,0:T(8,128)(2,1)} %resblocks.1) | data formatting | bytes 9437184

commit v3 on v2

--- a/solution.py
+++ b/solution.py
@@ -12,8 +12,11 @@
 LAYERS = 4
 LINE = 4
 NEAR = 2 * LINE
+CHUNK = 6
+EARLY = 3
 ROWS = 6
 UNROLL = 2
+STEP_ROWS = ROWS * UNROLL
 MESH = pl.DeviceIdType.MESH
 BF16 = jnp.bfloat16
 F32 = jnp.float32
@@ -70,12 +73,19 @@
 
     pl.semaphore_wait(barrier, NEAR - 1 + far - 1 + 2)
 
-    def halo_copy(src, slot):
-        return pltpu.make_async_remote_copy(src_ref=src.at[pl.ds(n_frames - 2, 2)], dst_ref=halo.at[slot], send_sem=halo_send.at[slot], recv_sem=halo_recv.at[slot], device_id={"cp": me + 1}, device_id_type=MESH)
-
-    @pl.when(me < n_dev - 1)
-    def _():
-        halo_copy(lat, 0).start()
+    n_chunks = height // CHUNK
+
+    def halo_copy(src, slot, chunk):
+        rows = pl.ds(chunk * CHUNK, CHUNK)
+        return pltpu.make_async_remote_copy(src_ref=src.at[pl.ds(n_frames - 2, 2), rows], dst_ref=halo.at[slot, :, rows], send_sem=halo_send.at[slot, chunk], recv_sem=halo_recv.at[slot, chunk], device_id={"cp": me + 1}, device_id_type=MESH)
+
+    def send_halo(src, slot, chunks):
+        @pl.when(me < n_dev - 1)
+        def _():
+            for chunk in chunks:
+                halo_copy(src, slot, chunk).start()
+
+    send_halo(lat, 0, range(EARLY))
 
     zero_row = jnp.zeros((width, chans), BF16)
     for f in range(n_frames + 2):
@@ -178,16 +188,17 @@
         half = normed * 0.5
         return (half + half * jnp.tanh(half)).astype(BF16)
 
-    def act_frames(src, frames, first):
+    def act_frames(src, frames, first, start=0, rows=height):
         def step(i, carry):
             for f in frames:
                 for r in range(2):
-                    act[first + f, 2 * i + r + 1] = act_rows(src[f, 2 * i + r])
+                    at = start + 2 * i + r
+                    act[first + f, at + 1] = act_rows(src[f, at])
             return carry
 
-        lax.fori_loop(0, height // 2, step, 0)
-
-    def conv_pair(layer, first, dst, residual, sums):
+        lax.fori_loop(0, rows // 2, step, 0)
+
+    def conv_pair(layer, first, dst, residual, sums, before=None):
         shift = bias[layer]
         zero_tile = jnp.zeros((chans, chans), BF16)
 
@@ -221,6 +232,8 @@
             return sums
 
         def step(i, sums):
+            if before is not None:
+                before(i)
             for u in range(UNROLL):
                 row = (i * UNROLL + u) * ROWS
                 block_pair(row)
@@ -233,25 +246,47 @@
         layer = 2 * block + odd
         src, dst = (mid, cur) if odd else (cur, mid)
         norm_coefs(layer, sums)
-        act_frames(src, range(n_frames), 2)
-        sums = conv_pair(layer, 2, dst, odd == 1, zero_sums)
-
-        def send_next():
-            @pl.when(me < n_dev - 1)
-            def _():
-                halo_copy(dst, 1 - odd).start()
+        in_step = STEP_ROWS // CHUNK
+        late = n_chunks - in_step
 
         if odd:
+            send_halo(src, odd, range(late, n_chunks))
+        else:
 
             @pl.when(block == 0)
             def _():
-                send_next()
+                send_halo(lat, odd, range(EARLY, n_chunks))
+
+            @pl.when(block > 0)
+            def _():
+                send_halo(src, odd, range(late, n_chunks))
+
+        act_frames(src, range(n_frames), 2)
+
+        def send_done_rows(i):
+            @pl.when((me < n_dev - 1) & (layer < LAYERS - 1) & (i > 0))
+            def _():
+                for c in range(in_step):
+                    halo_copy(dst, 1 - odd, (i - 1) * in_step + c).start()
+
+        sums = conv_pair(layer, 2, dst, odd == 1, zero_sums, send_done_rows)
+        if odd:
 
             @pl.when(block == 1)
             def _():
                 pltpu.make_async_copy(cur.at[pl.ds(2, 2)], out.at[pl.ds(2, 2)], out_sem.at[1]).start()
-        else:
-            send_next()
+
+        def take_chunk(chunk):
+            halo_copy(src, odd, chunk).wait_recv()
+            act_frames(halo.at[odd], range(2), 0, chunk * CHUNK, CHUNK)
+
+        def take_rows(i):
+            for c in range(in_step):
+                chunk = i * in_step + c + 1
+
+                @pl.when((me > 0) & (chunk < n_chunks))
+                def _():
+                    take_chunk(chunk)
 
         @pl.when(me == 0)
         def _():
@@ -264,14 +299,16 @@
 
         @pl.when(me > 0)
         def _():
-            halo_copy(src, odd).wait_recv()
-            act_frames(halo.at[odd], range(2), 0)
+            take_chunk(0)
+
+        sums = conv_pair(layer, 0, dst, odd == 1, sums, take_rows)
 
         @pl.when(me < n_dev - 1)
         def _():
-            halo_copy(src, odd).wait_send()
-
-        return conv_pair(layer, 0, dst, odd == 1, sums)
+            for chunk in range(n_chunks):
+                halo_copy(src, odd, chunk).wait_send()
+
+        return sums
 
     sums = zero_sums
     for f in range(n_frames):
@@ -324,8 +361,8 @@
                 dma((n_frames,)),
                 dma((LAYERS,)),
                 dma((2,)),
-                dma((2,)),
-                dma((2,)),
+                dma((2, height // CHUNK)),
+                dma((2, height // CHUNK)),
                 dma,
                 dma((LAYERS,)),
                 dma((LINE, 2)),

time: 200 us -> 191 us (0.955)
  Pallas kernels: 195 us -> 185 us
    pallas_call x1, Pallas kernels: 195 us -> 185 us  [local_fn(): pl.pallas_call(functools.partial(kernel, n_dev), out_shape=jax.ShapeDtype...]
where the time goes in v3:
time: 191 us
  Pallas kernels  185 us (97%)
  local copies, waits for them, and re-layouts  5.51 us (3%)
    pallas_call x1, Pallas kernels, local_fn(): pl.pallas_call(functools.partial(kernel, n_dev), out_shape=jax.ShapeDtype...  185 us
    unnamed x1, local copies, waits for them, and re-layouts  5.51 us

profile of v3, /device:TPU:1, one launch (start us, length us, event | category | flops | bytes accessed | tf_op | source)
XLA Modules:
  0.0 190.9 jit_solution(10520129778948759182)
XLA Ops:
  0.0 185.4 %resblocks.1 = bf16[4,48,96,128]{3,2,1,0:T(8,128)(2,1)} custom-call(bf16[4,48,96,128]{3,2,1,0:T(8,128)(2,1)} %refs_0_.1, bf16[4,3,3,3,128,128]{5,4,3,2,1,0:T(8,128)(2,1)} %refs_1_.1, f32[4,1,128]{2,1,0:T(1,128)} %bitcast.3, f32[4,1,128]{2,1,0:T(1,128)} %bitcast.4, f32[4,1,128]{2,1,0:T(1,128)} %bitcast.5), custom_call_target="tpu_custom_call" | custom-call | tf_op jit(solution)/shard_map/resblocks/pallas_call | solution.py:340
  185.4 5.5 %copy.7 = bf16[4,48,96,128]{3,2,1,0:T(8,128)(2,1)} copy(bf16[4,48,96,128]{3,2,1,0:T(8,128)(2,1)} %resblocks.1) | data formatting | bytes 9437184

commit v4 on v3

--- a/solution.py
+++ b/solution.py
@@ -55,23 +55,12 @@
         slot = lax.rem(far_pos + j, far)
         return slot, slot * NEAR + near_pos
 
-    barrier = pltpu.get_barrier_semaphore()
-    for j in range(1, NEAR):
-        pl.semaphore_signal(barrier, inc=1, device_id={"cp": near_base + lax.rem(near_pos + j, NEAR)}, device_id_type=MESH)
-    for j in range(1, far):
-        pl.semaphore_signal(barrier, inc=1, device_id={"cp": far_peer(j)[1]}, device_id_type=MESH)
-
-    for device in (lax.rem(me + 1, n_dev), lax.rem(me + n_dev - 1, n_dev)):
-        pl.semaphore_signal(barrier, inc=1, device_id={"cp": device}, device_id_type=MESH)
-
     frame_loads = [pltpu.make_async_copy(lat.at[f], cur.at[f], load_sem.at[f]) for f in range(n_frames)]
     for copy in frame_loads:
         copy.start()
     wts_loads = [pltpu.make_async_copy(kern.at[n], wts.at[n], wts_sem.at[n]) for n in range(LAYERS)]
     for copy in wts_loads:
         copy.start()
-
-    pl.semaphore_wait(barrier, NEAR - 1 + far - 1 + 2)
 
     n_chunks = height // CHUNK
 
@@ -370,7 +359,7 @@
                 dma((far,)),
                 dma((LAYERS, far)),
             ],
-            compiler_params=pltpu.CompilerParams(collective_id=0, has_side_effects=True, vmem_limit_bytes=60 * 1024 * 1024),
+            compiler_params=pltpu.CompilerParams(has_side_effects=True, vmem_limit_bytes=60 * 1024 * 1024),
             name="resblocks",
         )(latent, conv_kernels, conv_biases.reshape(row), gn_gammas.reshape(row), gn_betas.reshape(row))
 

time: 191 us -> 172 us (0.901)
  Pallas kernels: 185 us -> 166 us
    pallas_call x1, Pallas kernels: 185 us -> 166 us  [local_fn(): pl.pallas_call(functools.partial(kernel, n_dev), out_shape=jax.ShapeDtype...]
where the time goes in v4:
time: 172 us
  Pallas kernels  166 us (97%)
  local copies, waits for them, and re-layouts  5.51 us (3%)
    pallas_call x1, Pallas kernels, local_fn(): pl.pallas_call(functools.partial(kernel, n_dev), out_shape=jax.ShapeDtype...  166 us
    unnamed x1, local copies, waits for them, and re-layouts  5.51 us

profile of v4, /device:TPU:1, one launch (start us, length us, event | category | flops | bytes accessed | tf_op | source)
XLA Modules:
  0.0 171.9 jit_solution(14279739243931610506)
XLA Ops:
  0.0 166.4 %resblocks.1 = bf16[4,48,96,128]{3,2,1,0:T(8,128)(2,1)} custom-call(bf16[4,48,96,128]{3,2,1,0:T(8,128)(2,1)} %refs_0_.1, bf16[4,3,3,3,128,128]{5,4,3,2,1,0:T(8,128)(2,1)} %refs_1_.1, f32[4,1,128]{2,1,0:T(1,128)} %bitcast.3, f32[4,1,128]{2,1,0:T(1,128)} %bitcast.4, f32[4,1,128]{2,1,0:T(1,128)} %bitcast.5), custom_call_target="tpu_custom_call" | custom-call | tf_op jit(solution)/shard_map/resblocks/pallas_call | solution.py:329
  166.4 5.5 %copy.7 = bf16[4,48,96,128]{3,2,1,0:T(8,128)(2,1)} copy(bf16[4,48,96,128]{3,2,1,0:T(8,128)(2,1)} %resblocks.1) | data formatting | bytes 9437184
